TPU v7x, 32 devices: a whole 2x2x4 slice. The times are simulated.
32 devices in a mesh: row: 4 (over y, x), col: 8 (over z, core).
Axes of the slice: x: 2, y: 2, z: 4, core: 2. Of those that a mesh axis runs over, the one named last changes fastest.
Arguments:
- features: bfloat16 [8192, 512], P(('row', 'col')), may hold values from -40 to 40
- w_query: bfloat16 [512, 512], replicated, may hold values from -0.25 to 0.25
- w_key: bfloat16 [512, 512], replicated, may hold values from -0.25 to 0.25
- w_value: bfloat16 [512, 512], replicated, may hold values from -0.25 to 0.25
- w_out: bfloat16 [512, 512], replicated, may hold values from -0.25 to 0.25
- pairs: int32 [4, 8, 128, 2], P('row', 'col'), may hold values from 0 to 15, as said below
- counts: int32 [4, 8], P('row', 'col'), may hold values from 16 to 128, as said below
- masks: int32 [4, 8, 128, 128, 4], P('row', 'col'), may hold values from -2147483648 to 2147483646, as said below
Outputs:
- updated: bfloat16 [8192, 512], P(('row', 'col'))
Inputs may be any that keep to these rules, and one draw needn't show every extreme that they name: Within one device's list all 128 entries are distinct pairs; the first column is a query tile below 16, the second a key tile below 8. `counts`: some device has a full list of 128 entries in every draw. `masks`: any 32-bit pattern.
All inputs are finite; a program needn't handle non-finite values.
Results may differ from a plain program's by a relative error of at most 0.012.
The roundings to bfloat16 on the way count: a program that leaves them out, or rounds other values in their place, can miss the bound.
Values may be sent and summed in bfloat16 or wider, within the bound.
A program may use at most 128 MiB of HBM per device.

v0:
```python
import math

import jax
import jax.numpy as jnp
from jax import lax
from jax.sharding import PartitionSpec as P

HEADS = 8
TILE = 128


def merged(x, axis, combine):
    everything = jax.tree.map(lambda part: lax.all_gather(part, axis), x)
    initial = jax.tree.map(lambda part: part[0], everything)

    def step(k, so_far):
        return combine(so_far, jax.tree.map(lambda part: part[k], everything))

    return lax.fori_loop(1, lax.axis_size(axis), step, initial)


def unpack_bits(words):
    shifts = jnp.broadcast_to(jnp.arange(32, dtype=jnp.int32), words.shape + (32,))
    bits = lax.shift_right_logical(words[..., None], shifts) & 1
    return bits.reshape(words.shape[:-1] + (words.shape[-1] * 32,)) == 1


def body(features, w_query, w_key, w_value, w_out, pairs, counts, masks):
    nodes, width = features.shape
    heads = HEADS
    head_size = width // heads
    scale = 1.0 / math.sqrt(head_size)
    query_local = jnp.dot(features, w_query, preferred_element_type=jnp.float32).astype(
        jnp.bfloat16
    )
    queries = lax.all_gather(query_local, "col", axis=0, tiled=True)
    key_local = jnp.dot(features, w_key, preferred_element_type=jnp.float32).astype(jnp.bfloat16)
    value_local = jnp.dot(features, w_value, preferred_element_type=jnp.float32).astype(
        jnp.bfloat16
    )
    keys, values = (
        lax.all_gather(key_local, "row", axis=0, tiled=True),
        lax.all_gather(value_local, "row", axis=0, tiled=True),
    )
    q_tiles = queries.reshape(-1, TILE, width)
    k_tiles = keys.reshape(-1, TILE, width)
    v_tiles = values.reshape(-1, TILE, width)
    qtiles = q_tiles.shape[0]
    my_pairs = pairs[0, 0]
    my_count = counts[0, 0]
    my_words = masks[0, 0]
    per_turn = min(16, my_pairs.shape[0])
    turns = (my_count + per_turn - 1) // per_turn
    tile_ids = jnp.arange(qtiles, dtype=jnp.int32)

    def scores_of(turn):
        start = (turn * per_turn).astype(jnp.int32)
        block = lax.dynamic_slice_in_dim(my_pairs, start, per_turn, 0)
        words = lax.dynamic_slice_in_dim(my_words, start, per_turn, 0)
        q_blk = q_tiles[block[:, 0]].reshape(per_turn, TILE, heads, head_size)
        k_blk = k_tiles[block[:, 1]].reshape(per_turn, TILE, heads, head_size)
        scores = (
            jnp.einsum("gihd,gjhd->ghij", q_blk, k_blk, preferred_element_type=jnp.float32) * scale
        )
        valid = start + jnp.arange(per_turn, dtype=jnp.int32) < my_count
        live = unpack_bits(words) & valid[:, None, None]
        onehot = block[:, 0][:, None] == tile_ids[None, :]
        return (block, scores, live, onehot)

    def max_turn(turn, tile_max):
        block, scores, live, onehot = scores_of(turn)
        rowmax = jnp.where(live[:, None], scores, -jnp.inf).max(-1)
        candidate = jnp.where(onehot[:, :, None, None], rowmax[:, None], -jnp.inf).max(0)
        return jnp.maximum(tile_max, candidate)

    tile_max = lax.fori_loop(0, turns, max_turn, jnp.zeros((qtiles, heads, TILE), jnp.float32))

    def sum_turn(turn, carry):
        numer, total = carry
        block, scores, live, onehot = scores_of(turn)
        top = tile_max[block[:, 0]]
        prob = jnp.where(live[:, None], jnp.exp(scores - top[..., None]), 0.0).astype(jnp.bfloat16)
        selector = onehot.astype(jnp.float32)
        total = total + jnp.einsum(
            "gt,ghi->thi",
            selector,
            prob.astype(jnp.float32).sum(-1),
            precision=lax.Precision.HIGHEST,
        )
        v_blk = v_tiles[block[:, 1]].reshape(per_turn, TILE, heads, head_size)
        weighted = jnp.einsum(
            "ghij,gjhd->gihd", prob, v_blk, preferred_element_type=jnp.float32
        ).reshape(per_turn, TILE, width)
        numer = numer + jnp.einsum(
            "gt,gix->tix", selector, weighted, precision=lax.Precision.HIGHEST
        )
        return (numer, total)

    numer, total = lax.fori_loop(
        0,
        turns,
        sum_turn,
        (
            jnp.zeros((qtiles, TILE, width), jnp.float32),
            jnp.zeros((qtiles, heads, TILE), jnp.float32),
        ),
    )
    total = total + jnp.exp(-tile_max)
    rows = qtiles * TILE
    row_max = tile_max.transpose(0, 2, 1).reshape(rows, heads)
    row_den = total.transpose(0, 2, 1).reshape(rows, heads)
    row_part = (numer.reshape(rows, heads, head_size) / row_den[..., None]).astype(jnp.bfloat16)

    def combine(first, second):
        max_a, den_a = first
        max_b, den_b = second
        top = jnp.maximum(max_a, max_b)
        return (top, den_a * jnp.exp(max_a - top) + den_b * jnp.exp(max_b - top))

    whole_max, whole_den = merged((row_max, row_den), "col", combine)
    weight = jnp.exp(row_max - whole_max) * row_den
    term = (row_part.astype(jnp.float32) * weight[..., None]).reshape(rows, width)
    own_num = lax.psum_scatter(term, "col", scatter_dimension=0, tiled=True)
    offset = lax.axis_index("col") * nodes
    own_den = lax.dynamic_slice_in_dim(whole_den, offset, nodes, 0)
    attended = (
        (own_num.reshape(nodes, heads, head_size) / own_den[..., None])
        .astype(jnp.bfloat16)
        .reshape(nodes, width)
    )
    return jnp.dot(attended, w_out, preferred_element_type=jnp.float32).astype(jnp.bfloat16)


def solution(mesh):
    in_specs = (
        P(("row", "col"), None),
        P(),
        P(),
        P(),
        P(),
        P("row", "col", None, None),
        P("row", "col"),
        P("row", "col", None, None, None),
    )
    out_specs = P(("row", "col"), None)
    return jax.shard_map(body, mesh=mesh, in_specs=in_specs, out_specs=out_specs, check_vma=False)
```

profile of v0, /device:TPU:0, one launch (start us, length us, event | category | flops | bytes accessed | tf_op | source)
XLA Modules:
  0.0 717.4 jit_solution(805248537017498656)
XLA Ops:
  13.6 25.4 %all-gather.8.cloned.1.call-done = bf16[1024,512]{1,0:T(8,128)(2,1)} async-done(((bf16[256,512]{1,0:T(8,128)(2,1)}), bf16[1024,512]{1,0:T(8,128)(2,1)}) %all-gather.8.cloned.1.call-update) | async-done | bytes 1048592 | tf_op jit(solution)/shard_map/all_gather | solution.py:42
  38.9 30.8 %all-gather.6.cloned.1.call-done = bf16[2048,512]{1,0:T(8,128)(2,1)} async-done(((bf16[256,512]{1,0:T(8,128)(2,1)}), bf16[2048,512]{1,0:T(8,128)(2,1)}) %all-gather.6.cloned.1.call-update) | async-done | bytes 2097168 | tf_op jit(solution)/shard_map/all_gather | solution.py:36
  69.7 19.5 %while.42 = (s32[]{:T(128)}, f32[16,8,128]{2,1,0:T(8,128)S(1)}, s32[]{:T(128)}, s32[128,2]{0,1:T(2,128)S(1)}, s32[128,128,4]{1,2,0:T(4,128)}, /*index=5*/s32[]{:...) while((s32[]{:T(128)}, f32[16,8,128]{2,1,0:T(8,128)S(1)}, ...), condition=%wide.region_3.4_spmd.clone, body=%wide.region_0.3_spmd.clone.sunk | while | flops 276285824 | bytes 34582152 | solution.py:76
  69.8 3.6 gather_fusion
  73.4 4.0 copy.94
  79.4 4.0 copy.95
  85.4 3.4 select_reduce_fusion.4
  89.3 8.2 %all-gather.4.cloned.1.call-done = bf16[1024,512]{1,0:T(8,128)(2,1)} async-done(((bf16[256,512]{1,0:T(8,128)(2,1)}), bf16[1024,512]{1,0:T(8,128)(2,1)}) %all-gather.4.cloned.1.call-update) | async-done | bytes 1048592 | tf_op jit(solution)/shard_map/all_gather | solution.py:43
  100.0 47.3 %while.43 = (s32[]{:T(128)}, f32[16,128,512]{2,0,1:T(8,128)}, f32[16,8,128]{2,0,1:T(8,128)S(1)}, s32[]{:T(128)}, s32[128,2]{0,1:T(2,128)S(1)}, /*index=5*/bf16[8...) while((s32[]{:T(128)}, f32[16,128,512]{2,0,1:T(8,128)}, ...), condition=%wide.region_6.7_spmd.clone, body=%wide.region_4.6_spmd.clone.sunk | while | flops 756025984 | bytes 74493304 | solution.py:99
  100.3 3.6 gather_fusion.4
  104.0 3.9 copy.98
  109.9 3.9 copy.99
  116.3 7.0 convert_reduce_fusion.2
  125.4 3.0 copy.97
  128.4 5.4 fusion.71
  133.8 5.5 copy.100
  139.3 7.8 %convolution_add_fusion.4 = f32[16,128,512]{2,0,1:T(8,128)} fusion(f32[16,128,512]{2,0,1:T(8,128)} %get-tuple-element.632, f32[16,128,512]{2,0,1:T(8,128)} %copy.100, s32[16]{0:T(128)S(1)} %get-tuple-element.578), kind=kOutput, calls=%fused_computation.32.clone.1 | convolution fusion | flops 202375424 | bytes 12582976 | tf_op jit(solution)/shard_map/while/body/gt,gix->tix/dot_general | solution.py:94
  147.4 403.1 %all_gather.19 = f32[8,2048,8]{1,2,0:T(8,128)S(1)} all-gather(f32[1,2048,8]{1,2,0:T(8,128)S(1)} %all_gather_reshape.7), channel_id=1, replica_groups=mesh['row'=4,'col'=8] {'col'}, dimensions={0}, use_global_device_ids=true | all-gather | bytes 589824 | tf_op jit(solution)/shard_map/all_gather | solution.py:13
  550.5 14.8 %all_gather.18 = f32[8,2048,8]{1,2,0:T(8,128)S(1)} all-gather(f32[1,2048,8]{1,2,0:T(8,128)S(1)} %bitcast.161), channel_id=1, replica_groups=mesh['row'=4,'col'=8] {'col'}, dimensions={0}, use_global_device_ids=true | all-gather | bytes 589824 | tf_op jit(solution)/shard_map/all_gather | solution.py:13
  568.5 5.3 copy.68
  576.3 5.4 copy.67
  581.6 4.8 copy.65
  586.4 3.5 convert_multiply_fusion
  590.3 118.5 %reduce-scatter.2.cloned.1.call-done = f32[256,512]{1,0:T(8,128)} async-done(((f32[2048,512]{1,0:T(8,128)}), f32[256,512]{1,0:T(8,128)}) %reduce-scatter.2.cloned.1.call-update) | async-done | bytes 524304 | tf_op jit(solution)/shard_map/reduce_scatter | solution.py:123
  (86 shorter events, 28.4 us)
Async XLA Ops:
  6.5 1.0 copy-start
  6.5 5.3 copy-start.10
  6.5 5.3 copy-start.11
  6.5 63.2 %copy-start.12 = (s32[1,1,128,2]{2,3,1,0:T(2,128)S(1)}, s32[1,1,128,2]{2,3,1,0:T(2,128)}, u32[]{:S(2)}) copy-start(s32[1,1,128,2]{2,3,1,0:T(2,128)} %param.19) | copy-start | bytes 3076
  6.5 32.4 %all-gather.8.cloned.1.call-start = ((), (), s32[]{:S(2)}) async-start(), calls=%async_computation.3 | async-start | bytes 1310720 | tf_op jit(solution)/shard_map/all_gather | solution.py:42
  9.6 60.2 %all-gather.6.cloned.1.call-start = ((), (), s32[]{:S(2)}) async-start(), calls=%async_computation.2 | async-start | bytes 2359296 | tf_op jit(solution)/shard_map/all_gather | solution.py:36
  11.8 85.7 %all-gather.4.cloned.1.call-start = ((), (), s32[]{:S(2)}) async-start(), calls=%async_computation.1 | async-start | bytes 1310720 | tf_op jit(solution)/shard_map/all_gather | solution.py:43
  12.9 695.9 %reduce-scatter.2.cloned.1.call-start = ((), (), s32[]{:S(2)}) async-start(), calls=%async_computation.4 | async-start | bytes 4718592 | tf_op jit(solution)/shard_map/reduce_scatter | solution.py:123
  73.4 4.0 copy-start.2
  79.4 5.9 copy-start.7
  97.5 2.5 copy-start.3
  97.5 2.5 copy-start.5
  139.3 8.0 %copy-start.4 = (bf16[8,128,512]{2,1,0:T(8,128)(2,1)S(1)}, bf16[8,128,512]{2,1,0:T(8,128)(2,1)}, u32[]{:S(2)}) copy-start(bf16[8,128,512]{2,1,0:T(8,128)(2,1)} %get-tuple-element.706) | copy-start | bytes 3145732 | tf_op jit(solution)/shard_map/while
  139.3 8.0 %copy-start.6 = (bf16[1024,512]{1,0:T(8,128)(2,1)S(1)}, bf16[1024,512]{1,0:T(8,128)(2,1)}, u32[]{:S(2)}) copy-start(bf16[1024,512]{1,0:T(8,128)(2,1)} %get-tuple-element.726) | copy-start | bytes 3145732 | tf_op jit(solution)/shard_map/while
  581.6 4.8 copy-start.8
  581.6 4.8 copy-start.9
  589.9 118.9 %copy-start.13 = (bf16[512,512]{1,0:T(8,128)(2,1)S(1)}, bf16[512,512]{1,0:T(8,128)(2,1)}, u32[]{:S(2)}) copy-start(bf16[512,512]{1,0:T(8,128)(2,1)} %param.18) | copy-start | bytes 1572868
  590.0 120.9 %copy-start.1 = (bf16[512,512]{1,0:T(8,128)(2,1)S(1)}, bf16[512,512]{1,0:T(8,128)(2,1)}, u32[]{:S(2)}) copy-start(bf16[512,512]{1,0:T(8,128)(2,1)} %param.16) | copy-start | bytes 1572868
Sparse Core Ops, SparseCore 0:
  9.7 29.2 all-gather.7
  40.5 29.1 all-gather.5
  71.6 25.8 all-gather.3
  590.1 118.6 reduce-scatter.1
where the time goes:
time: 722 us; the launch traced here: 717 us
  blocking collectives  418 us (58%)
  waiting for transfers between devices  183 us (25%)
  local copies, waits for them, and re-layouts  64.5 us (9%)
  matrix products  31 us (4%)
  between operations  13.9 us (2%)
    all_gather x2, blocking collectives, merged(): everything = jax.tree.map(lambda part: lax.all_gather(part, axis), x)  418 us
    reduce_scatter x1, waiting for transfers between devices, body(): own_num = lax.psum_scatter(term, 'col', scatter_dimension=0, tiled=True)  119 us
    all_gather x1, waiting for transfers between devices, body(): queries = lax.all_gather(query_local, 'col', axis=0, tiled=True)  30.8 us
    all_gather x1, waiting for transfers between devices, body(): lax.all_gather(key_local, 'row', axis=0, tiled=True)  25.4 us
    gather x4, local copies, waits for them, and re-layouts, scores_of(): q_blk = q_tiles[block[:, 0]].reshape(per_turn, TILE, heads, head_size)  15.1 us
  transfers between devices with their start and end apart: 4, of which 4 were waited for; matrix products, arithmetic and copies ran while one was open for 3% of the time, Pallas kernels for 0%

commit v1 on v0

v1 whole, which is shorter than its diff:
```python
import functools
import math

import jax
import jax.numpy as jnp
from jax import lax
from jax.experimental import pallas as pl
from jax.experimental.pallas import tpu as pltpu
from jax.sharding import PartitionSpec as P

HEADS = 8
TILE = 128
BLOCK = 256
ONES = 16


def attend_group(
    group, table_ref, masks_ref, queries, k_ref, v_ref, part_ref, stat_ref, bias_ref, score_ref
):
    width, span = queries.shape
    keys = k_ref.shape[0]
    head = width // HEADS
    scale = 1.0 / math.sqrt(head)
    factor = scale * math.log2(math.e)
    k_tiles = keys // TILE
    tiles = span // TILE
    v_rows = v_ref.shape[0] // HEADS
    shift = 31 - lax.broadcasted_iota(jnp.int32, (32, TILE), 0)
    for b in range(k_tiles):
        for t in range(tiles):
            entry = table_ref[(group * tiles + t) * k_tiles + b]
            words = masks_ref[jnp.maximum(entry, 0)] * jnp.where(entry >= 0, 1, 0)
            for j in range(TILE // 32):
                bits = jnp.broadcast_to(words[j : j + 1, :], (32, TILE)) << shift
                bias_ref[pl.ds(b * TILE + j * 32, 32), pl.ds(t * TILE, TILE)] = jnp.where(
                    bits < 0, 0.0, -jnp.inf
                )
    step = min(BLOCK, keys)
    blocks = keys // step
    upper = lax.broadcasted_iota(jnp.int32, (2 * head, span), 0) < head

    def scores(h, block, top):
        pair = h // 2
        both = queries[pair * 2 * head : (pair + 1) * 2 * head, :]
        mine = jnp.where(upper == (h % 2 == 0), both, jnp.zeros_like(both))
        rows = slice(block * step, (block + 1) * step)
        raw = jnp.dot(
            k_ref[rows, pair * 2 * head : (pair + 1) * 2 * head],
            mine,
            preferred_element_type=jnp.float32,
        )
        raw = raw + bias_ref[rows, :]
        score_ref[h % 2, rows, :] = raw
        return jnp.maximum(top, jnp.max(raw.reshape(step // 8, 8, span), axis=0))

    def weighted(h, block, top, total):
        rows = slice(block * step, (block + 1) * step)
        prob = jnp.exp2((score_ref[h % 2, rows, :] - top) * factor).astype(jnp.bfloat16)
        term = jnp.dot(
            v_ref[h * v_rows : (h + 1) * v_rows, rows], prob, preferred_element_type=jnp.float32
        )
        return term if total is None else total + term

    def finish(h, top, total):
        peak = top * scale
        den = total[head : head + 1, :] + jnp.exp(-peak)
        part_ref[h * head : (h + 1) * head, :] = (total[:head, :] / den).astype(jnp.bfloat16)
        stat_ref[h : h + 1, :] = peak
        stat_ref[HEADS + h : HEADS + h + 1, :] = den

    zero = jnp.zeros((8, span), jnp.float32)
    tops = zero
    for block in range(blocks):
        tops = scores(0, block, tops)
    for h in range(HEADS):
        top = jnp.max(tops, axis=0, keepdims=True)
        total, tops = None, zero
        for block in range(blocks):
            if h + 1 < HEADS:
                tops = scores(h + 1, block, tops)
            total = weighted(h, block, top, total)
        finish(h, top, total)


def attention_kernel(table_ref, masks_ref, q_ref, k_ref, v_ref, part_ref, stat_ref, bias, score):
    attend_group(
        pl.program_id(0),
        table_ref,
        masks_ref,
        q_ref.at[0],
        k_ref,
        v_ref,
        part_ref.at[0],
        stat_ref.at[0],
        bias,
        score,
    )


def attention(table, masks, q_all, k_part, v_part):
    groups, width, span = q_all.shape
    keys = k_part.shape[0]
    whole = pl.BlockSpec(memory_space=pltpu.VMEM)
    return pl.pallas_call(
        attention_kernel,
        grid=(groups,),
        out_shape=(
            jax.ShapeDtypeStruct((groups, width, span), jnp.bfloat16),
            jax.ShapeDtypeStruct((groups, 2 * HEADS, span), jnp.float32),
        ),
        in_specs=[
            pl.BlockSpec(memory_space=pltpu.SMEM),
            whole,
            pl.BlockSpec((1, width, span), lambda g: (g, 0, 0)),
            whole,
            whole,
        ],
        out_specs=(
            pl.BlockSpec((1, width, span), lambda g: (g, 0, 0)),
            pl.BlockSpec((1, 2 * HEADS, span), lambda g: (g, 0, 0)),
        ),
        scratch_shapes=[
            pltpu.VMEM((keys, span), jnp.float32),
            pltpu.VMEM((2, keys, span), jnp.float32),
        ],
        compiler_params=pltpu.CompilerParams(
            dimension_semantics=("arbitrary",), vmem_limit_bytes=48 * 1024 * 1024
        ),
        name="attention",
    )(table, masks, q_all, k_part, v_part)


def entry_table(pairs, count, q_tiles, k_tiles):
    entries = pairs.shape[0]
    ids = lax.broadcasted_iota(jnp.int32, (q_tiles * k_tiles, entries), 1)
    cell = lax.broadcasted_iota(jnp.int32, (q_tiles * k_tiles, entries), 0)
    code = (pairs[:, 0] * k_tiles + pairs[:, 1])[None, :]
    return jnp.max(jnp.where((code == cell) & (ids < count), ids, -1), axis=1)


def body(features, w_query, w_key, w_value, w_out, pairs, counts, masks):
    nodes, width = features.shape
    head = width // HEADS
    f32 = jnp.float32
    gathered = lax.all_gather(features, "row", axis=0, tiled=True)
    q_local = lax.dot_general(
        w_query, features, (((0,), (1,)), ((), ())), preferred_element_type=f32
    ).astype(jnp.bfloat16)
    q_all = lax.all_gather(q_local, "col", axis=0)
    k_part = jnp.dot(gathered, w_key, preferred_element_type=f32).astype(jnp.bfloat16)
    v_part = lax.dot_general(
        w_value, gathered, (((0,), (1,)), ((), ())), preferred_element_type=f32
    ).astype(jnp.bfloat16)
    keys = k_part.shape[0]
    v_part = jnp.concatenate(
        [v_part.reshape(HEADS, head, keys), jnp.ones((HEADS, ONES, keys), jnp.bfloat16)], axis=1
    ).reshape(HEADS * (head + ONES), keys)
    groups = q_all.shape[0]
    table = entry_table(pairs[0, 0], counts[0, 0], groups * nodes // TILE, keys // TILE)
    words = masks[0, 0].transpose(0, 2, 1)
    part, stat = attention(table, words, q_all, k_part, v_part)
    part = lax.all_to_all(part, "col", 0, 0)
    stat = lax.all_to_all(stat, "col", 0, 0)
    peak, den = stat[:, :HEADS], stat[:, HEADS:]
    top = jnp.max(peak, axis=0)
    weight = jnp.exp(peak - top) * den
    total = weight.sum(0)
    numer = (part.reshape(groups, HEADS, head, nodes).astype(f32) * weight[:, :, None, :]).sum(0)
    attended = (numer / total[:, None, :]).astype(jnp.bfloat16).reshape(width, nodes)
    return lax.dot_general(
        attended, w_out, (((0,), (0,)), ((), ())), preferred_element_type=f32
    ).astype(jnp.bfloat16)


def solution(mesh):
    in_specs = (
        P(("row", "col"), None),
        P(),
        P(),
        P(),
        P(),
        P("row", "col", None, None),
        P("row", "col"),
        P("row", "col", None, None, None),
    )
    out_specs = P(("row", "col"), None)
    return jax.shard_map(body, mesh=mesh, in_specs=in_specs, out_specs=out_specs, check_vma=False)
```

time: 722 us -> 170 us (0.24)
  blocking collectives: 418 us -> 9.56 us
  waiting for transfers between devices: 183 us -> 105 us
  local copies, waits for them, and re-layouts: 64.5 us -> 1.49 us
  Pallas kernels: 0 us -> 28.5 us
  matrix products: 31 us -> 5.99 us
    all_gather x2 -> x0, blocking collectives: 418 us -> none  [merged(): everything = jax.tree.map(lambda part: lax.all_gather(part, axis), x)]
    reduce_scatter x1 -> x0, waiting for transfers between devices: 119 us -> none  [body(): own_num = lax.psum_scatter(term, 'col', scatter_dimension=0, tiled=True)]
    all_to_all x0 -> x1, waiting for transfers between devices: none -> 48.9 us  [body(): part = lax.all_to_all(part, 'col', 0, 0)]
    gather x11 -> x0, local copies, waits for them, and re-layouts: 32.8 us -> none  [the longest x4 15.1 us: scores_of(): q_blk = q_tiles[block[:, 0]].reshape(per_turn, TILE, heads, head_size)]
    pallas_call x0 -> x1, Pallas kernels: none -> 28.5 us  [attention(): pl.pallas_call(attention_kernel, grid=(groups,), out_shape=(jax.ShapeDtyp...]
    dot_general x9 -> x4, matrix products: 31 us -> 5.99 us  [the longest x1 2.16 us: body(): lax.dot_general(w_query, features, (((0,), (1,)), ((), ())), preferred_el...]
    all_to_all x0 -> x1, blocking collectives: none -> 9.56 us  [body(): stat = lax.all_to_all(stat, 'col', 0, 0)]
    all_gather x3 -> x2, waiting for transfers between devices: 64.4 us -> 55.2 us  [the longest x1 27.8 us: body(): q_all = lax.all_gather(q_local, 'col', axis=0)]
  transfers between devices with their start and end apart: 4 -> 3, of which waited for: 4 -> 3; matrix products, arithmetic and copies ran while one was open for 3% -> 4% of each run, Pallas kernels for 0% -> 0%
where the time goes in v1:
time: 170 us
  waiting for transfers between devices  105 us (62%)
  Pallas kernels  28.5 us (17%)
  between operations  14.2 us (8%)
  blocking collectives  9.56 us (6%)
  matrix products  5.99 us (4%)
  starting transfers between devices  3.64 us (2%)
    all_to_all x1, waiting for transfers between devices, body(): part = lax.all_to_all(part, 'col', 0, 0)  48.9 us
    pallas_call x1, Pallas kernels, attention(): pl.pallas_call(attention_kernel, grid=(groups,), out_shape=(jax.ShapeDtyp...  28.5 us
    all_gather x1, waiting for transfers between devices, body(): q_all = lax.all_gather(q_local, 'col', axis=0)  27.8 us
    all_gather x1, waiting for transfers between devices, body(): gathered = lax.all_gather(features, 'row', axis=0, tiled=True)  27.4 us
    all_to_all x1, blocking collectives, body(): stat = lax.all_to_all(stat, 'col', 0, 0)  9.56 us
    all_to_all x1, starting transfers between devices, body(): part = lax.all_to_all(part, 'col', 0, 0)  3.6 us
  transfers between devices with their start and end apart: 3, of which 3 were waited for; matrix products, arithmetic and copies ran while one was open for 4% of the time, Pallas kernels for 0%

profile of v1, /device:TPU:0, one launch (start us, length us, event | category | flops | bytes accessed | tf_op | source)
XLA Modules:
  0.0 169.5 jit_solution(13695341005512216223)
XLA Ops:
  6.5 0.0 copy-start
  6.5 0.0 all-gather.4.cloned.1.call-start
  6.5 0.7 all-gather.4.cloned.1.call-update
  7.3 0.0 all-gather.6.cloned.1.call-start
  7.3 2.2 %convolution_convert_fusion.3 = bf16[512,256]{1,0:T(8,128)(2,1)} fusion(bf16[512,512]{1,0:T(8,128)(2,1)} %param.9, bf16[256,512]{1,0:T(8,128)(2,1)} %param.8), kind=kOutput, calls=%fused_computation.5 | convolution fusion | flops 134348800 | bytes 1048576 | tf_op jit(solution)/shard_map/dot_general | solution.py:146
  9.5 0.0 all-gather.6.cloned.1.call-update
  10.1 0.8 add_bitcast_fusion
  10.9 0.1 select_reduce_fusion.table_ref
  11.0 27.4 %all-gather.4.cloned.1.call-done = bf16[1024,512]{1,0:T(8,128)(2,1)} async-done(((bf16[256,512]{1,0:T(8,128)(2,1)}), bf16[1024,512]{1,0:T(8,128)(2,1)}) %all-gather.4.cloned.1.call-update) | async-done | bytes 1048592 | tf_op jit(solution)/shard_map/all_gather | solution.py:145
  38.4 0.0 copy-done
  38.4 2.1 %convolution_convert_fusion = bf16[512,1024]{1,0:T(8,128)(2,1)S(1)} fusion(bf16[512,512]{1,0:T(8,128)(2,1)S(1)} %copy-done, bf16[1024,512]{1,0:T(8,128)(2,1)} %all-gather.4.cloned.1.call-done), kind=kOutput, calls=%fused_computation.2 | convolution fusion | flops 537395200 | bytes 2621440 | tf_op jit(solution)/shard_map/dot_general | solution.py:151
  40.5 0.0 copy-start.2
  40.6 0.1 concatenate.3
  40.7 0.7 convolution_convert_fusion.1.k_ref
  41.4 27.8 %all-gather.6.cloned.1.call-done = bf16[4096,256]{1,0:T(8,128)(2,1)} async-done(((bf16[512,256]{1,0:T(8,128)(2,1)}), bf16[4096,256]{1,0:T(8,128)(2,1)}) %all-gather.6.cloned.1.call-update) | async-done | bytes 2097168 | tf_op jit(solution)/shard_map/all_gather | solution.py:149
  69.2 28.5 %attention.1 = (bf16[8,512,256]{2,1,0:T(8,128)(2,1)S(1)}, f32[8,16,256]{2,1,0:T(8,128)S(1)}) custom-call(s32[128]{0:T(128)S(1)} %select_reduce_fusion.table_ref, s32[128,4,128]{2,1,0:T(4,128)S(1)} %bitcast.28, bf16[8,512,256]{2,1,0:T(8,128)(2,1)} %bitcast.29, bf16[1024,512]{1,0:T(8,128)(2,1)S(1)} %convolution_convert_fusion.1.k_ref, ...), custom_call_target="tpu_custom_call" | custom-call | tf_op jit(solution)/shard_map/attention/pallas_call | solution.py:104
  97.7 1.3 copy-done.1
  99.0 9.6 %all_to_all.10 = f32[8,16,256]{2,1,0:T(8,128)S(1)} all-to-all(f32[8,16,256]{2,1,0:T(8,128)S(1)} %get-tuple-element.8), channel_id=1, replica_groups=mesh['row'=4,'col'=8] {'col'}, dimensions={0} | all-to-all | bytes 262144 | tf_op jit(solution)/shard_map/all_to_all | solution.py:163
  108.6 3.6 %all-to-all-start = ((bf16[8,512,256]{2,1,0:T(8,128)(2,1)}), bf16[8,512,256]{2,1,0:T(8,128)(2,1)S(1)}, u32[]{:S(2)}, u32[]{:S(2)}) async-start(bf16[8,512,256]{2,1,0:T(8,128)(2,1)} %copy-done.1), calls=%async_computation | async-start | bytes 4194304 | tf_op jit(solution)/shard_map/all_to_all | solution.py:162
  112.2 0.0 copy-start.3
  112.2 48.9 %all-to-all-done = bf16[8,512,256]{2,1,0:T(8,128)(2,1)S(1)} async-done(((bf16[8,512,256]{2,1,0:T(8,128)(2,1)}), bf16[8,512,256]{2,1,0:T(8,128)(2,1)S(1)}, u32[]{:S(2)}, u32[]{:S(2)}) %all-to-all-start) | async-done | bytes 2097184 | tf_op jit(solution)/shard_map/all_to_all | solution.py:162
  161.1 0.4 fusion
  161.6 0.1 fusion.1
  161.6 1.0 convolution_convert_fusion.2
  (10 shorter events, 0.1 us)
Async XLA Ops:
  6.5 31.9 %copy-start = (bf16[512,512]{1,0:T(8,128)(2,1)S(1)}, bf16[512,512]{1,0:T(8,128)(2,1)}, u32[]{:S(2)}) copy-start(bf16[512,512]{1,0:T(8,128)(2,1)} %param.11) | copy-start | bytes 1572868
  6.5 31.9 %all-gather.4.cloned.1.call-start = ((), (), s32[]{:S(2)}) async-start(), calls=%async_computation.2 | async-start | bytes 1310720 | tf_op jit(solution)/shard_map/all_gather | solution.py:145
  7.3 62.0 %all-gather.6.cloned.1.call-start = ((), (), s32[]{:S(2)}) async-start(), calls=%async_computation.3 | async-start | bytes 2359296 | tf_op jit(solution)/shard_map/all_gather | solution.py:149
  38.4 2.3 %copy-start.4 = (bf16[1024,512]{1,0:T(8,128)(2,1)S(1)}, bf16[1024,512]{1,0:T(8,128)(2,1)}, u32[]{:S(2)}) copy-start(bf16[1024,512]{1,0:T(8,128)(2,1)} %all-gather.4.cloned.1.call-done) | copy-start | bytes 3145732
  38.4 2.3 %copy-start.5 = (bf16[512,512]{1,0:T(8,128)(2,1)S(1)}, bf16[512,512]{1,0:T(8,128)(2,1)}, u32[]{:S(2)}) copy-start(bf16[512,512]{1,0:T(8,128)(2,1)} %param.10) | copy-start | bytes 1572868
  40.5 28.7 %copy-start.2 = (s32[1,1,128,128,4]{3,4,2,1,0:T(4,128)S(1)}, s32[1,1,128,128,4]{3,4,2,1,0:T(4,128)}, u32[]{:S(2)}) copy-start(s32[1,1,128,128,4]{3,4,2,1,0:T(4,128)} %param.15) | copy-start | bytes 786436
  97.7 1.3 copy-start.1
  108.6 52.6 %all-to-all-start = ((bf16[8,512,256]{2,1,0:T(8,128)(2,1)}), bf16[8,512,256]{2,1,0:T(8,128)(2,1)S(1)}, u32[]{:S(2)}, u32[]{:S(2)}) async-start(bf16[8,512,256]{2,1,0:T(8,128)(2,1)} %copy-done.1), calls=%async_computation | async-start | bytes 4194304 | tf_op jit(solution)/shard_map/all_to_all | solution.py:162
  112.2 49.5 %copy-start.3 = (bf16[512,512]{1,0:T(8,128)(2,1)S(1)}, bf16[512,512]{1,0:T(8,128)(2,1)}, u32[]{:S(2)}) copy-start(bf16[512,512]{1,0:T(8,128)(2,1)} %param.12) | copy-start | bytes 1572868
Sparse Core Ops, SparseCore 0:
  9.2 29.2 all-gather.3
  40.0 29.1 all-gather.5

commit v2 on v1

v2 whole, which is shorter than its diff:
```python
import functools
import math

import jax
import jax.numpy as jnp
from jax import lax
from jax.experimental import pallas as pl
from jax.experimental.pallas import tpu as pltpu
from jax.sharding import PartitionSpec as P

HEADS = 8
TILE = 128
BLOCK = 256
ONES = 16


def attend_group(
    group, table_ref, masks_ref, queries, k_ref, v_ref, part_ref, stat_ref, bias_ref, score_ref
):
    width, span = queries.shape
    keys = k_ref.shape[0]
    head = width // HEADS
    scale = 1.0 / math.sqrt(head)
    factor = scale * math.log2(math.e)
    k_tiles = keys // TILE
    tiles = span // TILE
    v_rows = v_ref.shape[0] // HEADS
    shift = 31 - lax.broadcasted_iota(jnp.int32, (32, TILE), 0)
    for b in range(k_tiles):
        for t in range(tiles):
            entry = table_ref[(group * tiles + t) * k_tiles + b]
            words = masks_ref[jnp.maximum(entry, 0)] * jnp.where(entry >= 0, 1, 0)
            for j in range(TILE // 32):
                bits = jnp.broadcast_to(words[j : j + 1, :], (32, TILE)) << shift
                bias_ref[pl.ds(b * TILE + j * 32, 32), pl.ds(t * TILE, TILE)] = jnp.where(
                    bits < 0, 0.0, -jnp.inf
                )
    step = min(BLOCK, keys)
    blocks = keys // step
    upper = lax.broadcasted_iota(jnp.int32, (2 * head, span), 0) < head

    def scores(h, block, top):
        pair = h // 2
        both = queries[pair * 2 * head : (pair + 1) * 2 * head, :]
        mine = jnp.where(upper == (h % 2 == 0), both, jnp.zeros_like(both))
        rows = slice(block * step, (block + 1) * step)
        raw = jnp.dot(
            k_ref[rows, pair * 2 * head : (pair + 1) * 2 * head],
            mine,
            preferred_element_type=jnp.float32,
        )
        raw = raw + bias_ref[rows, :]
        score_ref[h % 2, rows, :] = raw
        return jnp.maximum(top, jnp.max(raw.reshape(step // 8, 8, span), axis=0))

    def weighted(h, block, top, total):
        rows = slice(block * step, (block + 1) * step)
        prob = jnp.exp2((score_ref[h % 2, rows, :] - top) * factor).astype(jnp.bfloat16)
        term = jnp.dot(
            v_ref[h * v_rows : (h + 1) * v_rows, rows], prob, preferred_element_type=jnp.float32
        )
        return term if total is None else total + term

    def finish(h, top, total):
        peak = top * scale
        den = total[head : head + 1, :] + jnp.exp(-peak)
        part_ref[h * head : (h + 1) * head, :] = (total[:head, :] / den).astype(jnp.bfloat16)
        stat_ref[h : h + 1, :] = peak
        stat_ref[HEADS + h : HEADS + h + 1, :] = den

    zero = jnp.zeros((8, span), jnp.float32)
    tops = zero
    for block in range(blocks):
        tops = scores(0, block, tops)
    for h in range(HEADS):
        top = jnp.max(tops, axis=0, keepdims=True)
        total, tops = None, zero
        for block in range(blocks):
            if h + 1 < HEADS:
                tops = scores(h + 1, block, tops)
            total = weighted(h, block, top, total)
        finish(h, top, total)


MESH = pl.DeviceIdType.MESH


def fused_kernel(
    rows,
    cols,
    table_ref,
    masks_ref,
    features_ref,
    wq_ref,
    wk_ref,
    wv_ref,
    wo_ref,
    out_ref,
    frow,
    fcol,
    wq_t,
    wv_t,
    k_all,
    v_all,
    q_now,
    part,
    stat,
    pair_part,
    pair_stat,
    both_part,
    both_stat,
    fin_part,
    fin_stat,
    bias,
    score,
    row_send,
    row_recv,
    col_recv,
    right_send,
    left_send,
    share_left,
    share_right,
    pair_send,
    pair_recv,
    fin_send,
    fin_recv,
):
    nodes, width = features_ref.shape
    head = width // HEADS
    f32 = jnp.float32
    chips = cols // 2
    r, c = lax.axis_index("row"), lax.axis_index("col")
    m, k = c // 2, lax.rem(c, 2)
    mate = (r, m * 2 + 1 - k)

    def at(chip):
        return (r, chip * 2 + k)

    def send(src, dst, send_sem, recv_sem, device):
        return pltpu.make_async_remote_copy(
            src_ref=src,
            dst_ref=dst,
            send_sem=send_sem,
            recv_sem=recv_sem,
            device_id=device,
            device_id_type=MESH,
        )

    barrier = pltpu.get_barrier_semaphore()
    pl.semaphore_signal(barrier, inc=1, device_id=mate, device_id_type=MESH)
    for d in range(1, rows):
        peer = (lax.rem(r + d, rows), c)
        pl.semaphore_signal(barrier, inc=1, device_id=peer, device_id_type=MESH)
    for d in range(1, chips):
        peer = at(lax.rem(m + d, chips))
        pl.semaphore_signal(barrier, inc=1, device_id=peer, device_id_type=MESH)
    pl.semaphore_wait(barrier, 1 + rows - 1 + chips - 1)

    has_right, has_left = m + 1 < chips, m >= 1

    def to_right(s):
        slot = (m - s) * 2 + k
        src = features_ref if s == 0 else fcol.at[slot]
        return send(src, fcol.at[slot], right_send.at[s], col_recv.at[slot], at(m + 1))

    def to_left(s):
        slot = (m + s) * 2 + k
        src = features_ref if s == 0 else fcol.at[slot]
        return send(src, fcol.at[slot], left_send.at[s], col_recv.at[slot], at(m - 1))

    def to_mate_left(s):
        slot = (m - s) * 2 + k
        src = features_ref if s == 0 else fcol.at[slot]
        return send(src, fcol.at[slot], share_left.at[s], col_recv.at[slot], mate)

    def to_mate_right(s):
        slot = (m + s) * 2 + k
        return send(fcol.at[slot], fcol.at[slot], share_right.at[s], col_recv.at[slot], mate)

    def to_row(d):
        return send(
            features_ref, frow.at[r], row_send.at[d], row_recv.at[r], (lax.rem(r + d, rows), c)
        )

    def await_col(slot):
        send(fcol.at[slot], fcol.at[slot], right_send.at[0], col_recv.at[slot], mate).wait_recv()

    @pl.when(has_right)
    def _():
        to_right(0).start()

    @pl.when(has_left)
    def _():
        to_left(0).start()

    for d in range(1, rows):
        to_row(d).start()
    to_mate_left(0).start()

    frow[r] = features_ref[...]
    fcol[c] = features_ref[...]
    wq_t[...] = wq_ref[...].T
    wv_t[...] = wv_ref[...].T
    for h in range(HEADS):
        v_all[h * (head + ONES) + head : (h + 1) * (head + ONES), :] = jnp.ones(
            (ONES, rows * nodes), jnp.bfloat16
        )

    def project_row(slot):
        block = frow[slot]
        lane = pl.ds(pl.multiple_of(slot * nodes, nodes), nodes)
        k_all[lane, :] = jnp.dot(block, wk_ref[...], preferred_element_type=f32).astype(
            jnp.bfloat16
        )
        value = lax.dot_general(
            wv_t[...], block, (((1,), (1,)), ((), ())), preferred_element_type=f32
        ).astype(jnp.bfloat16)
        for h in range(HEADS):
            v_all[h * (head + ONES) : h * (head + ONES) + head, lane] = value[
                h * head : (h + 1) * head, :
            ]

    project_row(r)
    for s in range(1, chips):
        if s == chips - 1:
            for d in range(1, rows):
                slot = lax.rem(r + rows - d, rows)
                send(
                    frow.at[slot], frow.at[slot], row_send.at[0], row_recv.at[slot], mate
                ).wait_recv()
                project_row(slot)

        @pl.when(m >= s)
        def _():
            await_col((m - s) * 2 + k)
            to_mate_left(s).start()
            if s + 1 < chips:

                @pl.when(has_right)
                def _():
                    to_right(s).start()

        @pl.when(m + s < chips)
        def _():
            await_col((m + s) * 2 + k)
            to_mate_right(s).start()
            if s + 1 < chips:

                @pl.when(has_left)
                def _():
                    to_left(s).start()

    def pair_copies(i, j):
        return (
            send(part.at[i], pair_part.at[j], pair_send.at[j, 0], pair_recv.at[j, 0], mate),
            send(stat.at[i], pair_stat.at[j], pair_send.at[j, 1], pair_recv.at[j, 1], mate),
        )

    def fin_copies(j):
        owner = at(lax.rem(m + 1 + j, chips))
        return (
            send(both_part.at[j], fin_part.at[j], fin_send.at[j, 0], fin_recv.at[j, 0], owner),
            send(both_stat.at[j], fin_stat.at[j], fin_send.at[j, 1], fin_recv.at[j, 1], owner),
        )

    def weigh(sources):
        peaks = [ref[0:HEADS, :] for _, ref in sources]
        top = functools.reduce(jnp.maximum, peaks)
        weights = [
            jnp.exp(peak - top) * ref[HEADS : 2 * HEADS, :]
            for peak, (_, ref) in zip(peaks, sources)
        ]
        total = functools.reduce(jnp.add, weights)
        return top, weights, total

    def blend(sources, weights, total, h):
        rows_of = slice(h * head, (h + 1) * head)
        numer = functools.reduce(
            jnp.add,
            [
                ref[rows_of, :].astype(f32) * weight[h : h + 1, :]
                for weight, (ref, _) in zip(weights, sources)
            ],
        )
        return (numer / total[h : h + 1, :]).astype(jnp.bfloat16)

    def merge(j):
        for copy in pair_copies(0, j):
            copy.wait_recv()
        mine = 2 * j + k
        sources = [(part.at[mine], stat.at[mine]), (pair_part.at[j], pair_stat.at[j])]
        top, weights, total = weigh(sources)
        both_stat[j, 0:HEADS, :] = top
        both_stat[j, HEADS : 2 * HEADS, :] = total
        for h in range(HEADS):
            both_part[j, h * head : (h + 1) * head, :] = blend(sources, weights, total, h)
        for copy in fin_copies(j):
            copy.start()

    def turn(i, carry):
        j = i // 2
        odd = lax.rem(i, 2)
        chip = lax.rem(m + 1 + j, chips)
        group = chip * 2 + odd

        @pl.when(odd != k)
        def _():
            await_col(group)

        q_now[...] = lax.dot_general(
            wq_t[...], fcol[group], (((1,), (1,)), ((), ())), preferred_element_type=f32
        ).astype(jnp.bfloat16)
        attend_group(
            group,
            table_ref,
            masks_ref,
            q_now,
            k_all,
            v_all,
            part.at[i],
            stat.at[i],
            bias,
            score,
        )

        @pl.when(odd != k)
        def _():
            for copy in pair_copies(i, j):
                copy.start()

        @pl.when((odd == 0) & (i > 0))
        def _():
            merge(j - 1)

        return carry

    lax.fori_loop(0, cols, turn, 0)

    last = chips - 1
    mine = 2 * last + k
    for copy in pair_copies(0, last):
        copy.wait_recv()
    for j in range(last):
        for copy in fin_copies(j):
            copy.wait_recv()
    sources = [(part.at[mine], stat.at[mine]), (pair_part.at[last], pair_stat.at[last])]
    sources += [(fin_part.at[j], fin_stat.at[j]) for j in range(last)]
    _, weights, total = weigh(sources)
    for h in range(HEADS):
        q_now[h * head : (h + 1) * head, :] = blend(sources, weights, total, h)
    out_ref[...] = lax.dot_general(
        q_now[...], wo_ref[...], (((0,), (0,)), ((), ())), preferred_element_type=f32
    ).astype(jnp.bfloat16)

    for d in range(1, rows):
        to_row(d).wait_send()
    to_mate_left(0).wait_send()
    for s in range(chips):

        @pl.when(m >= s)
        def _():
            if s > 0:
                to_mate_left(s).wait_send()
            if s + 1 < chips:

                @pl.when(has_right)
                def _():
                    to_right(s).wait_send()

        @pl.when(m + s < chips)
        def _():
            if s > 0:
                to_mate_right(s).wait_send()
            if s + 1 < chips:

                @pl.when(has_left)
                def _():
                    to_left(s).wait_send()

    for j in range(chips):
        for copy in pair_copies(0, j):
            copy.wait_send()
    for j in range(last):
        for copy in fin_copies(j):
            copy.wait_send()


def fused(mesh_shape, table, masks, features, w_query, w_key, w_value, w_out):
    rows, cols = mesh_shape["row"], mesh_shape["col"]
    chips = cols // 2
    nodes, width = features.shape
    keys = rows * nodes
    head = width // HEADS
    bf16, f32 = jnp.bfloat16, jnp.float32
    whole = pl.BlockSpec(memory_space=pltpu.VMEM)
    dma = pltpu.SemaphoreType.DMA
    return pl.pallas_call(
        functools.partial(fused_kernel, rows, cols),
        out_shape=jax.ShapeDtypeStruct((nodes, width), bf16),
        in_specs=[pl.BlockSpec(memory_space=pltpu.SMEM)] + [whole] * 6,
        out_specs=whole,
        scratch_shapes=[
            pltpu.VMEM((rows, nodes, width), bf16),
            pltpu.VMEM((cols, nodes, width), bf16),
            pltpu.VMEM((width, width), bf16),
            pltpu.VMEM((width, width), bf16),
            pltpu.VMEM((keys, width), bf16),
            pltpu.VMEM((HEADS * (head + ONES), keys), bf16),
            pltpu.VMEM((width, nodes), bf16),
            pltpu.VMEM((cols, width, nodes), bf16),
            pltpu.VMEM((cols, 2 * HEADS, nodes), f32),
            pltpu.VMEM((chips, width, nodes), bf16),
            pltpu.VMEM((chips, 2 * HEADS, nodes), f32),
            pltpu.VMEM((chips, width, nodes), bf16),
            pltpu.VMEM((chips, 2 * HEADS, nodes), f32),
            pltpu.VMEM((chips, width, nodes), bf16),
            pltpu.VMEM((chips, 2 * HEADS, nodes), f32),
            pltpu.VMEM((keys, nodes), f32),
            pltpu.VMEM((2, keys, nodes), f32),
            dma((rows,)),
            dma((rows,)),
            dma((cols,)),
            dma((chips,)),
            dma((chips,)),
            dma((chips,)),
            dma((chips,)),
            dma((chips, 2)),
            dma((chips, 2)),
            dma((chips, 2)),
            dma((chips, 2)),
        ],
        compiler_params=pltpu.CompilerParams(
            collective_id=0, has_side_effects=True, vmem_limit_bytes=60 * 1024 * 1024
        ),
        name="fused",
    )(table, masks, features, w_query, w_key, w_value, w_out)


def entry_table(pairs, count, q_tiles, k_tiles):
    entries = pairs.shape[0]
    ids = lax.broadcasted_iota(jnp.int32, (q_tiles * k_tiles, entries), 1)
    cell = lax.broadcasted_iota(jnp.int32, (q_tiles * k_tiles, entries), 0)
    code = (pairs[:, 0] * k_tiles + pairs[:, 1])[None, :]
    return jnp.max(jnp.where((code == cell) & (ids < count), ids, -1), axis=1)


def body(mesh_shape, features, w_query, w_key, w_value, w_out, pairs, counts, masks):
    nodes = features.shape[0]
    rows, cols = mesh_shape["row"], mesh_shape["col"]
    table = entry_table(pairs[0, 0], counts[0, 0], cols * nodes // TILE, rows * nodes // TILE)
    words = masks[0, 0].transpose(0, 2, 1)
    return fused(mesh_shape, table, words, features, w_query, w_key, w_value, w_out)


def solution(mesh):
    in_specs = (
        P(("row", "col"), None),
        P(),
        P(),
        P(),
        P(),
        P("row", "col", None, None),
        P("row", "col"),
        P("row", "col", None, None, None),
    )
    out_specs = P(("row", "col"), None)
    return jax.shard_map(
        functools.partial(body, dict(mesh.shape)), mesh=mesh, in_specs=in_specs, out_specs=out_specs, check_vma=False)
```

time: 170 us -> 69.1 us (0.41)
  the two profiles are of different devices: /device:TPU:0 before, /device:TPU:9 now
where the time goes in v2:
time: 69.1 us; the launch traced here: 68.9 us
  Pallas kernels  65.2 us (94%)
  local copies, waits for them, and re-layouts  2.34 us (3%)
    pallas_call x1, Pallas kernels, fused(): pl.pallas_call(functools.partial(fused_kernel, rows, cols), out_shape=jax...  65.2 us
    unnamed x3, local copies, waits for them, and re-layouts  2.34 us

profile of v2, /device:TPU:9, one launch (start us, length us, event | category | flops | bytes accessed | tf_op | source)
XLA Modules:
  0.0 68.9 jit_solution(10117341604370119840)
XLA Ops:
  0.7 0.0 copy-start
  0.7 0.7 copy-done
  1.4 0.6 select_reduce_fusion.table_ref
  2.0 65.2 %fused.1 = bf16[256,512]{1,0:T(8,128)(2,1)} custom-call(s32[128]{0:T(128)} %select_reduce_fusion.table_ref, s32[128,4,128]{2,1,0:T(4,128)} %bitcast.8, bf16[256,512]{1,0:T(8,128)(2,1)} %features_ref.1, bf16[512,512]{1,0:T(8,128)(2,1)} %wq_ref.1, bf16[512,512]{1,0:T(8,128)(2,1)} %wk_ref.1, bf16[512,512]{1,0:T(8,128)(2,1)} %wv_ref.1, bf16[512,512]{1,0:T(8,128)(2,1)} %wo_ref.1), custom_call_target="tpu_custom_call" | custom-call | tf_op jit(solution)/shard_map/fused/pallas_call | solution.py:397
  67.2 1.7 %copy.11 = bf16[256,512]{1,0:T(8,128)(2,1)} copy(bf16[256,512]{1,0:T(8,128)(2,1)} %fused.1) | data formatting | bytes 524288
  (2 shorter events, 0.0 us)
Async XLA Ops:
  0.7 0.7 copy-start

commit v3 on v2

--- a/solution.py
+++ b/solution.py
@@ -14,17 +14,10 @@
 ONES = 16
 
 
-def attend_group(
-    group, table_ref, masks_ref, queries, k_ref, v_ref, part_ref, stat_ref, bias_ref, score_ref
-):
-    width, span = queries.shape
-    keys = k_ref.shape[0]
-    head = width // HEADS
-    scale = 1.0 / math.sqrt(head)
-    factor = scale * math.log2(math.e)
+def build_bias(group, table_ref, masks_ref, bias_ref):
+    keys, span = bias_ref.shape
     k_tiles = keys // TILE
     tiles = span // TILE
-    v_rows = v_ref.shape[0] // HEADS
     shift = 31 - lax.broadcasted_iota(jnp.int32, (32, TILE), 0)
     for b in range(k_tiles):
         for t in range(tiles):
@@ -35,6 +28,15 @@
                 bias_ref[pl.ds(b * TILE + j * 32, 32), pl.ds(t * TILE, TILE)] = jnp.where(
                     bits < 0, 0.0, -jnp.inf
                 )
+
+
+def attend_group(queries, k_ref, v_ref, part_ref, stat_ref, bias_ref, score_ref):
+    width, span = queries.shape
+    keys = k_ref.shape[0]
+    head = width // HEADS
+    scale = 1.0 / math.sqrt(head)
+    factor = scale * math.log2(math.e)
+    v_rows = v_ref.shape[0] // HEADS
     step = min(BLOCK, keys)
     blocks = keys // step
     upper = lax.broadcasted_iota(jnp.int32, (2 * head, span), 0) < head
@@ -94,7 +96,6 @@
     wq_ref,
     wk_ref,
     wv_ref,
-    wo_ref,
     out_ref,
     frow,
     fcol,
@@ -133,8 +134,26 @@
     m, k = c // 2, lax.rem(c, 2)
     mate = (r, m * 2 + 1 - k)
 
+    half = chips // 2
+
     def at(chip):
         return (r, chip * 2 + k)
+
+    def owner_chip(j):
+        return lax.rem(m + jnp.where(j == 0, half, jnp.where(j < half, j, j + 1)), chips)
+
+    def flip(place, b):
+        return place + 1 - 2 * lax.rem(place, 2) if b else place
+
+    def row_to(d):
+        if rows % 2:
+            return lax.rem(r + d, rows)
+        return flip(lax.rem(r + d // 2 * 2, rows), d % 2)
+
+    def row_from(d):
+        if rows % 2:
+            return lax.rem(r + rows - d, rows)
+        return lax.rem(flip(r, d % 2) + rows - d // 2 * 2, rows)
 
     def send(src, dst, send_sem, recv_sem, device):
         return pltpu.make_async_remote_copy(
@@ -179,7 +198,7 @@
 
     def to_row(d):
         return send(
-            features_ref, frow.at[r], row_send.at[d], row_recv.at[r], (lax.rem(r + d, rows), c)
+            features_ref, frow.at[r], row_send.at[d], row_recv.at[r], (row_to(d), c)
         )
 
     def await_col(slot):
@@ -221,15 +240,13 @@
             ]
 
     project_row(r)
-    for s in range(1, chips):
-        if s == chips - 1:
-            for d in range(1, rows):
-                slot = lax.rem(r + rows - d, rows)
-                send(
-                    frow.at[slot], frow.at[slot], row_send.at[0], row_recv.at[slot], mate
-                ).wait_recv()
-                project_row(slot)
-
+
+    def await_row(d):
+        slot = row_from(d)
+        send(frow.at[slot], frow.at[slot], row_send.at[0], row_recv.at[slot], mate).wait_recv()
+        project_row(slot)
+
+    def relay(s):
         @pl.when(m >= s)
         def _():
             await_col((m - s) * 2 + k)
@@ -249,6 +266,15 @@
                 @pl.when(has_left)
                 def _():
                     to_left(s).start()
+
+    late = min(chips - half + 1, chips)
+    for s in range(1, late):
+        relay(s)
+        if s == 1:
+            for d in range(1, rows - 1):
+                await_row(d)
+    for d in range(rows - 1 if chips > 1 and late > 1 else 1, rows):
+        await_row(d)
 
     def pair_copies(i, j):
         return (
@@ -257,7 +283,7 @@
         )
 
     def fin_copies(j):
-        owner = at(lax.rem(m + 1 + j, chips))
+        owner = at(owner_chip(j))
         return (
             send(both_part.at[j], fin_part.at[j], fin_send.at[j, 0], fin_recv.at[j, 0], owner),
             send(both_stat.at[j], fin_stat.at[j], fin_send.at[j, 1], fin_recv.at[j, 1], owner),
@@ -300,8 +326,12 @@
     def turn(i, carry):
         j = i // 2
         odd = lax.rem(i, 2)
-        chip = lax.rem(m + 1 + j, chips)
-        group = chip * 2 + odd
+        group = owner_chip(j) * 2 + odd
+
+        @pl.when(i == 1)
+        def _():
+            for s in range(late, chips):
+                relay(s)
 
         @pl.when(odd != k)
         def _():
@@ -310,25 +340,20 @@
         q_now[...] = lax.dot_general(
             wq_t[...], fcol[group], (((1,), (1,)), ((), ())), preferred_element_type=f32
         ).astype(jnp.bfloat16)
-        attend_group(
-            group,
-            table_ref,
-            masks_ref,
-            q_now,
-            k_all,
-            v_all,
-            part.at[i],
-            stat.at[i],
-            bias,
-            score,
-        )
+        build_bias(group, table_ref, masks_ref, bias)
+
+        @pl.when((i == cols - 2) & (i > 0))
+        def _():
+            merge(j - 1)
+
+        attend_group(q_now, k_all, v_all, part.at[i], stat.at[i], bias, score)
 
         @pl.when(odd != k)
         def _():
             for copy in pair_copies(i, j):
                 copy.start()
 
-        @pl.when((odd == 0) & (i > 0))
+        @pl.when((odd == 0) & (i > 0) & (i < cols - 2))
         def _():
             merge(j - 1)
 
@@ -347,10 +372,7 @@
     sources += [(fin_part.at[j], fin_stat.at[j]) for j in range(last)]
     _, weights, total = weigh(sources)
     for h in range(HEADS):
-        q_now[h * head : (h + 1) * head, :] = blend(sources, weights, total, h)
-    out_ref[...] = lax.dot_general(
-        q_now[...], wo_ref[...], (((0,), (0,)), ((), ())), preferred_element_type=f32
-    ).astype(jnp.bfloat16)
+        out_ref[h * head : (h + 1) * head, :] = blend(sources, weights, total, h)
 
     for d in range(1, rows):
         to_row(d).wait_send()
@@ -385,7 +407,7 @@
             copy.wait_send()
 
 
-def fused(mesh_shape, table, masks, features, w_query, w_key, w_value, w_out):
+def fused(mesh_shape, table, masks, features, w_query, w_key, w_value):
     rows, cols = mesh_shape["row"], mesh_shape["col"]
     chips = cols // 2
     nodes, width = features.shape
@@ -396,8 +418,8 @@
     dma = pltpu.SemaphoreType.DMA
     return pl.pallas_call(
         functools.partial(fused_kernel, rows, cols),
-        out_shape=jax.ShapeDtypeStruct((nodes, width), bf16),
-        in_specs=[pl.BlockSpec(memory_space=pltpu.SMEM)] + [whole] * 6,
+        out_shape=jax.ShapeDtypeStruct((width, nodes), bf16),
+        in_specs=[pl.BlockSpec(memory_space=pltpu.SMEM)] + [whole] * 5,
         out_specs=whole,
         scratch_shapes=[
             pltpu.VMEM((rows, nodes, width), bf16),
@@ -433,7 +455,7 @@
             collective_id=0, has_side_effects=True, vmem_limit_bytes=60 * 1024 * 1024
         ),
         name="fused",
-    )(table, masks, features, w_query, w_key, w_value, w_out)
+    )(table, masks, features, w_query, w_key, w_value)
 
 
 def entry_table(pairs, count, q_tiles, k_tiles):
@@ -449,7 +471,10 @@
     rows, cols = mesh_shape["row"], mesh_shape["col"]
     table = entry_table(pairs[0, 0], counts[0, 0], cols * nodes // TILE, rows * nodes // TILE)
     words = masks[0, 0].transpose(0, 2, 1)
-    return fused(mesh_shape, table, words, features, w_query, w_key, w_value, w_out)
+    attended = fused(mesh_shape, table, words, features, w_query, w_key, w_value)
+    return lax.dot_general(
+        attended, w_out, (((0,), (0,)), ((), ())), preferred_element_type=jnp.float32
+    ).astype(jnp.bfloat16)
 
 
 def solution(mesh):

time: 69.1 us -> 65.9 us (0.954)
  the two profiles are of different devices: /device:TPU:9 before, /device:TPU:0 now
where the time goes in v3:
time: 65.9 us; the launch traced here: 65.8 us
  Pallas kernels  61.7 us (94%)
  matrix products  1.98 us (3%)
  between operations  0.74 us (1%)
  local copies, waits for them, and re-layouts  0.68 us (1%)
    pallas_call x1, Pallas kernels, fused(): pl.pallas_call(functools.partial(fused_kernel, rows, cols), out_shape=jax...  61.7 us
    dot_general x1, matrix products, body(): lax.dot_general(attended, w_out, (((0,), (0,)), ((), ())), preferred_elem...  1.98 us

profile of v3, /device:TPU:0, one launch (start us, length us, event | category | flops | bytes accessed | tf_op | source)
XLA Modules:
  0.0 65.8 jit_solution(6764752957788512854)
XLA Ops:
  0.0 0.0 copy-start
  0.7 0.0 copy-start.1
  0.7 0.7 %copy-done.1 = s32[1,1,128,2]{2,3,1,0:T(2,128)S(1)} copy-done((s32[1,1,128,2]{2,3,1,0:T(2,128)S(1)}, s32[1,1,128,2]{2,3,1,0:T(2,128)}, u32[]{:S(2)}) %copy-start.1) | copy-done | bytes 1048
  1.4 0.6 select_reduce_fusion.table_ref
  2.0 61.7 %fused.1 = bf16[512,256]{1,0:T(8,128)(2,1)} custom-call(s32[128]{0:T(128)} %select_reduce_fusion.table_ref, s32[128,4,128]{2,1,0:T(4,128)} %bitcast.10, bf16[256,512]{1,0:T(8,128)(2,1)} %features_ref.1, bf16[512,512]{1,0:T(8,128)(2,1)} %wq_ref.1, bf16[512,512]{1,0:T(8,128)(2,1)} %wk_ref.1, bf16[512,512]{1,0:T(8,128)(2,1)} %wv_ref.1), custom_call_target="tpu_custom_call" | custom-call | tf_op jit(solution)/shard_map/fused/pallas_call | solution.py:419
  63.8 0.0 copy-done
  63.8 2.0 %convolution_convert_fusion = bf16[256,512]{1,0:T(8,128)(2,1)} fusion(bf16[512,256]{1,0:T(8,128)(2,1)} %fused.1, bf16[512,512]{1,0:T(8,128)(2,1)S(1)} %copy-done), kind=kOutput, calls=%fused_computation | convolution fusion | flops 134348800 | bytes 1048576 | tf_op jit(solution)/shard_map/dot_general | solution.py:475
  (2 shorter events, 0.0 us)
Async XLA Ops:
  0.0 63.8 %copy-start = (bf16[512,512]{1,0:T(8,128)(2,1)S(1)}, bf16[512,512]{1,0:T(8,128)(2,1)}, u32[]{:S(2)}) copy-start(bf16[512,512]{1,0:T(8,128)(2,1)} %param.12) | copy-start | bytes 1572868
  0.7 0.7 %copy-start.1 = (s32[1,1,128,2]{2,3,1,0:T(2,128)S(1)}, s32[1,1,128,2]{2,3,1,0:T(2,128)}, u32[]{:S(2)}) copy-start(s32[1,1,128,2]{2,3,1,0:T(2,128)} %param.13) | copy-start | bytes 3076

commit v4 on v3

--- a/solution.py
+++ b/solution.py
@@ -10,8 +10,9 @@
 
 HEADS = 8
 TILE = 128
-BLOCK = 256
+BLOCK = 512
 ONES = 16
+CHUNKS = 2
 
 
 def build_bias(group, table_ref, masks_ref, bias_ref):
@@ -177,44 +178,48 @@
 
     has_right, has_left = m + 1 < chips, m >= 1
 
-    def to_right(s):
-        slot = (m - s) * 2 + k
-        src = features_ref if s == 0 else fcol.at[slot]
-        return send(src, fcol.at[slot], right_send.at[s], col_recv.at[slot], at(m + 1))
-
-    def to_left(s):
-        slot = (m + s) * 2 + k
-        src = features_ref if s == 0 else fcol.at[slot]
-        return send(src, fcol.at[slot], left_send.at[s], col_recv.at[slot], at(m - 1))
-
-    def to_mate_left(s):
-        slot = (m - s) * 2 + k
-        src = features_ref if s == 0 else fcol.at[slot]
-        return send(src, fcol.at[slot], share_left.at[s], col_recv.at[slot], mate)
-
-    def to_mate_right(s):
-        slot = (m + s) * 2 + k
-        return send(fcol.at[slot], fcol.at[slot], share_right.at[s], col_recv.at[slot], mate)
+    def hop(slot, own, piece, send_sem, device):
+        size = nodes // CHUNKS
+        span = pl.ds(piece * size, size)
+        src = features_ref.at[span] if own else fcol.at[slot, span]
+        return send(
+            src, fcol.at[slot, span], send_sem.at[piece], col_recv.at[slot, piece], device
+        )
+
+    def to_right(s, piece):
+        return hop((m - s) * 2 + k, s == 0, piece, right_send.at[s], at(m + 1))
+
+    def to_left(s, piece):
+        return hop((m + s) * 2 + k, s == 0, piece, left_send.at[s], at(m - 1))
+
+    def to_mate_left(s, piece):
+        return hop((m - s) * 2 + k, s == 0, piece, share_left.at[s], mate)
+
+    def to_mate_right(s, piece):
+        return hop((m + s) * 2 + k, s == 0, piece, share_right.at[s], mate)
 
     def to_row(d):
         return send(
             features_ref, frow.at[r], row_send.at[d], row_recv.at[r], (row_to(d), c)
         )
 
-    def await_col(slot):
-        send(fcol.at[slot], fcol.at[slot], right_send.at[0], col_recv.at[slot], mate).wait_recv()
-
-    @pl.when(has_right)
-    def _():
-        to_right(0).start()
-
-    @pl.when(has_left)
-    def _():
-        to_left(0).start()
+    def await_col(slot, piece):
+        hop(slot, False, piece, right_send.at[0], mate).wait_recv()
+
+    for piece in range(CHUNKS):
+
+        @pl.when(has_right)
+        def _():
+            to_right(0, piece).start()
+
+        @pl.when(has_left)
+        def _():
+            to_left(0, piece).start()
 
     for d in range(1, rows):
         to_row(d).start()
-    to_mate_left(0).start()
+    for piece in range(CHUNKS):
+        to_mate_left(0, piece).start()
 
     frow[r] = features_ref[...]
     fcol[c] = features_ref[...]
@@ -247,25 +252,29 @@
         project_row(slot)
 
     def relay(s):
-        @pl.when(m >= s)
-        def _():
-            await_col((m - s) * 2 + k)
-            to_mate_left(s).start()
-            if s + 1 < chips:
-
-                @pl.when(has_right)
-                def _():
-                    to_right(s).start()
-
-        @pl.when(m + s < chips)
-        def _():
-            await_col((m + s) * 2 + k)
-            to_mate_right(s).start()
-            if s + 1 < chips:
-
-                @pl.when(has_left)
-                def _():
-                    to_left(s).start()
+        for piece in range(CHUNKS):
+
+            @pl.when(m >= s)
+            def _():
+                await_col((m - s) * 2 + k, piece)
+                if s + 1 < chips:
+
+                    @pl.when(has_right)
+                    def _():
+                        to_right(s, piece).start()
+
+                to_mate_left(s, piece).start()
+
+            @pl.when(m + s < chips)
+            def _():
+                await_col((m + s) * 2 + k, piece)
+                if s + 1 < chips:
+
+                    @pl.when(has_left)
+                    def _():
+                        to_left(s, piece).start()
+
+                to_mate_right(s, piece).start()
 
     late = min(chips - half + 1, chips)
     for s in range(1, late):
@@ -328,21 +337,22 @@
         odd = lax.rem(i, 2)
         group = owner_chip(j) * 2 + odd
 
-        @pl.when(i == 1)
+        @pl.when(i == min(2, cols - 1))
         def _():
             for s in range(late, chips):
                 relay(s)
 
         @pl.when(odd != k)
         def _():
-            await_col(group)
+            for piece in range(CHUNKS):
+                await_col(group, piece)
 
         q_now[...] = lax.dot_general(
             wq_t[...], fcol[group], (((1,), (1,)), ((), ())), preferred_element_type=f32
         ).astype(jnp.bfloat16)
         build_bias(group, table_ref, masks_ref, bias)
 
-        @pl.when((i == cols - 2) & (i > 0))
+        @pl.when((odd == 0) & (i > 0))
         def _():
             merge(j - 1)
 
@@ -352,10 +362,6 @@
         def _():
             for copy in pair_copies(i, j):
                 copy.start()
-
-        @pl.when((odd == 0) & (i > 0) & (i < cols - 2))
-        def _():
-            merge(j - 1)
 
         return carry
 
@@ -376,28 +382,27 @@
 
     for d in range(1, rows):
         to_row(d).wait_send()
-    to_mate_left(0).wait_send()
     for s in range(chips):
-
-        @pl.when(m >= s)
-        def _():
-            if s > 0:
-                to_mate_left(s).wait_send()
-            if s + 1 < chips:
-
-                @pl.when(has_right)
-                def _():
-                    to_right(s).wait_send()
-
-        @pl.when(m + s < chips)
-        def _():
-            if s > 0:
-                to_mate_right(s).wait_send()
-            if s + 1 < chips:
-
-                @pl.when(has_left)
-                def _():
-                    to_left(s).wait_send()
+        for piece in range(CHUNKS):
+
+            @pl.when(m >= s)
+            def _():
+                to_mate_left(s, piece).wait_send()
+                if s + 1 < chips:
+
+                    @pl.when(has_right)
+                    def _():
+                        to_right(s, piece).wait_send()
+
+            @pl.when(m + s < chips)
+            def _():
+                if s > 0:
+                    to_mate_right(s, piece).wait_send()
+                if s + 1 < chips:
+
+                    @pl.when(has_left)
+                    def _():
+                        to_left(s, piece).wait_send()
 
     for j in range(chips):
         for copy in pair_copies(0, j):
@@ -441,11 +446,11 @@
             pltpu.VMEM((2, keys, nodes), f32),
             dma((rows,)),
             dma((rows,)),
-            dma((cols,)),
-            dma((chips,)),
-            dma((chips,)),
-            dma((chips,)),
-            dma((chips,)),
+            dma((cols, CHUNKS)),
+            dma((chips, CHUNKS)),
+            dma((chips, CHUNKS)),
+            dma((chips, CHUNKS)),
+            dma((chips, CHUNKS)),
             dma((chips, 2)),
             dma((chips, 2)),
             dma((chips, 2)),

time: 65.9 us -> 61 us (0.926)
  Pallas kernels: 61.7 us -> 56.8 us
    pallas_call x1, Pallas kernels: 61.7 us -> 56.8 us  [fused(): pl.pallas_call(functools.partial(fused_kernel, rows, cols), out_shape=jax...]
where the time goes in v4:
time: 61 us; the launch traced here: 60.8 us
  Pallas kernels  56.8 us (93%)
  matrix products  1.98 us (3%)
  between operations  0.74 us (1%)
  local copies, waits for them, and re-layouts  0.68 us (1%)
  other arithmetic  0.64 us (1%)
    pallas_call x1, Pallas kernels, fused(): pl.pallas_call(functools.partial(fused_kernel, rows, cols), out_shape=jax...  56.8 us
    dot_general x1, matrix products, body(): lax.dot_general(attended, w_out, (((0,), (0,)), ((), ())), preferred_elem...  1.98 us

profile of v4, /device:TPU:0, one launch (start us, length us, event | category | flops | bytes accessed | tf_op | source)
XLA Modules:
  0.0 60.8 jit_solution(3053469805660892799)
XLA Ops:
  0.0 0.0 copy-start
  0.7 0.0 copy-start.1
  0.7 0.7 %copy-done.1 = s32[1,1,128,2]{2,3,1,0:T(2,128)S(1)} copy-done((s32[1,1,128,2]{2,3,1,0:T(2,128)S(1)}, s32[1,1,128,2]{2,3,1,0:T(2,128)}, u32[]{:S(2)}) %copy-start.1) | copy-done | bytes 1048
  1.4 0.6 %select_reduce_fusion.table_ref = s32[128]{0:T(128)} fusion(s32[128]{0:T(128)S(1)} %add_bitcast_fusion, pred[128]{0:T(512)(128)(4,1)S(1)} %iota_compare_fusion.1), kind=kLoop, calls=%fused_computation.1 | loop fusion | flops 65408 | bytes 1152 | tf_op jit(solution)/shard_map/reduce_max | solution.py:471
  2.0 56.8 %fused.1 = bf16[512,256]{1,0:T(8,128)(2,1)} custom-call(s32[128]{0:T(128)} %select_reduce_fusion.table_ref, s32[128,4,128]{2,1,0:T(4,128)} %bitcast.10, bf16[256,512]{1,0:T(8,128)(2,1)} %features_ref.1, bf16[512,512]{1,0:T(8,128)(2,1)} %wq_ref.1, bf16[512,512]{1,0:T(8,128)(2,1)} %wk_ref.1, bf16[512,512]{1,0:T(8,128)(2,1)} %wv_ref.1), custom_call_target="tpu_custom_call" | custom-call | tf_op jit(solution)/shard_map/fused/pallas_call | solution.py:424
  58.8 0.0 copy-done
  58.8 2.0 %convolution_convert_fusion = bf16[256,512]{1,0:T(8,128)(2,1)} fusion(bf16[512,256]{1,0:T(8,128)(2,1)} %fused.1, bf16[512,512]{1,0:T(8,128)(2,1)S(1)} %copy-done), kind=kOutput, calls=%fused_computation | convolution fusion | flops 134348800 | bytes 1048576 | tf_op jit(solution)/shard_map/dot_general | solution.py:480
  (2 shorter events, 0.0 us)
Async XLA Ops:
  0.0 58.8 %copy-start = (bf16[512,512]{1,0:T(8,128)(2,1)S(1)}, bf16[512,512]{1,0:T(8,128)(2,1)}, u32[]{:S(2)}) copy-start(bf16[512,512]{1,0:T(8,128)(2,1)} %param.12) | copy-start | bytes 1572868
  0.7 0.7 %copy-start.1 = (s32[1,1,128,2]{2,3,1,0:T(2,128)S(1)}, s32[1,1,128,2]{2,3,1,0:T(2,128)}, u32[]{:S(2)}) copy-start(s32[1,1,128,2]{2,3,1,0:T(2,128)} %param.13) | copy-start | bytes 3076
